TPU v7x, 32 devices: a 4x4x1 block of a 4x4x8 slice. The times are simulated.
32 devices in a mesh: batch: 1 (over z), rows: 4 (over y), ksplit: 8 (over x, core).
Axes of the slice: x: 4, y: 4, z: 1, core: 2. Of those that a mesh axis runs over, the one named last changes fastest.
The devices are a block of a 4x4x8 slice.
Arguments:
- a_vals: bfloat16 [4, 8, 12, 128, 128], P(('batch', 'rows'), 'ksplit')
- b_vals: bfloat16 [8, 72, 128, 128], P(('batch', 'ksplit'))
- pairs: int32 [4, 8, 432, 1, 2], P(('batch', 'rows'), 'ksplit')
- plist_idx: int32 [4, 8, 432, 2], P(('batch', 'rows'), 'ksplit')
- c_idx: int32 [4, 8, 72, 2], P(('batch', 'rows'), 'ksplit')
Outputs:
- output: float32 [4, 8, 72, 128, 128], P(('batch', 'rows'), 'ksplit')
All inputs are finite; a program needn't handle non-finite values.
Results may differ from a plain program's by a relative error of at most 0.001.
Values are sent between devices in bfloat16 or wider.
A program may use at most 768 MiB of HBM per device.

v0:
```python
import jax
import jax.numpy as jnp
from jax import lax
from jax.sharding import PartitionSpec as P


def solution(mesh):
    row_spec = P(('batch', 'rows'), 'ksplit')
    col_spec = P(('batch', 'ksplit'))

    def device_step(a_loc, b_loc, pair_loc, plist_loc, cidx_loc):
        a_blocks = a_loc[0, 0]
        b_blocks = b_loc[0]
        pair_tab = pair_loc[0, 0]
        own_idx = cidx_loc[0, 0]
        block_size = a_blocks.shape[-1]
        a_sel = jnp.take(a_blocks, pair_tab[:, :, 0], axis=0)
        b_sel = jnp.take(b_blocks, pair_tab[:, :, 1], axis=0)
        part_sums = jnp.einsum('stab,stbc->sac', a_sel, b_sel, preferred_element_type=jnp.float32).astype(jnp.bfloat16)
        recv_vals = lax.all_to_all(part_sums, 'ksplit', 0, 0, tiled=True)
        recv_idx = lax.all_to_all(plist_loc[0, 0], 'ksplit', 0, 0, tiled=True)
        hit_mask = jnp.all(own_idx[:, None, :] == recv_idx[None, :, :], axis=-1).astype(jnp.bfloat16)
        flat_vals = recv_vals.reshape(recv_vals.shape[0], block_size * block_size)
        c_flat = jnp.dot(hit_mask, flat_vals, preferred_element_type=jnp.float32)
        return c_flat.reshape(1, 1, own_idx.shape[0], block_size, block_size)

    return jax.shard_map(device_step, mesh=mesh, in_specs=(row_spec, col_spec, row_spec, row_spec, row_spec), out_specs=row_spec, check_vma=False)
```

profile of v0, /device:TPU:97, one launch (start us, length us, event | category | flops | bytes accessed | tf_op | source)
XLA Modules:
  0.0 231.2 jit_solution(2863732978491732752)
XLA Ops:
  0.0 0.0 copy-start
  0.0 0.9 all_to_all.9
  0.9 0.6 copy.22
  1.5 6.0 %all-to-all-start = ((s32[8,54,2]{1,2,0:T(2,128)}), s32[8,54,2]{1,2,0:T(2,128)S(1)}, u32[]{:S(2)}, u32[]{:S(2)}) async-start(s32[8,54,2]{1,2,0:T(2,128)} %copy.22), calls=%async_computation | async-start | bytes 16384 | tf_op jit(solution)/shard_map/all_to_all | solution.py:21
  7.5 0.8 and_reduce_fusion.1
  8.4 14.1 %gather_fusion = bf16[432,128,128]{2,1,0:T(8,128)(2,1)} fusion(bf16[12,128,128]{2,1,0:T(8,128)(2,1)} %bitcast.31, s32[1024]{0:T(1024)S(1)} %pad_clamp_fusion.1), kind=kCustom, calls=%fused_computation | custom fusion | bytes 28313280 | tf_op jit(solution)/shard_map/jit(_take)/gather | solution.py:17
  22.4 0.0 copy-done
  22.4 13.2 %gather_fusion.1 = bf16[432,128,128]{2,1,0:T(8,128)(2,1)} fusion(bf16[72,128,128]{2,1,0:T(8,128)(2,1)S(1)} %bitcast.30, s32[1024]{0:T(1024)S(1)} %pad_clamp_fusion), kind=kCustom, calls=%fused_computation.1 | custom fusion | bytes 28313280 | tf_op jit(solution)/shard_map/jit(_take)/gather | solution.py:18
  35.7 16.4 %fusion.8 = bf16[432,128,128]{2,1,0:T(8,128)(2,1)} fusion(bf16[432,128,128]{2,1,0:T(8,128)(2,1)} %gather_fusion.1, pred[432]{0:T(512)(128)(4,1)S(1)} %get-tuple-element.9, bf16[432,128,128]{2,1,0:T(8,128)(2,1)} %gather_fusion, pred[432]{0:T(512)(128)(4,1)S(1)} %get-tuple-element.5), kind=kOutput, calls=%fused_computation.11 | convolution fusion | flops 1833172992 | bytes 42468192 | tf_op jit(solution)/shard_map/stab,stbc->sac/dot_general | solution.py:19
  52.1 0.0 copy-start.2
  52.1 0.0 all-to-all-done
  52.1 5.9 %all-to-all-start.1 = ((bf16[432,128,128]{2,1,0:T(8,128)(2,1)}), bf16[432,128,128]{2,1,0:T(8,128)(2,1)}, u32[]{:S(2)}, u32[]{:S(2)}) async-start(bf16[432,128,128]{2,1,0:T(8,128)(2,1)} %fusion.8), calls=%async_computation.1 | async-start | bytes 28311552 | tf_op jit(solution)/shard_map/all_to_all | solution.py:20
  58.0 0.1 eq.19
  58.1 0.0 copy-done.2
  58.1 0.1 compare_reduce_fusion
  58.2 154.8 %all-to-all-done.1 = bf16[432,128,128]{2,1,0:T(8,128)(2,1)} async-done(((bf16[432,128,128]{2,1,0:T(8,128)(2,1)}), bf16[432,128,128]{2,1,0:T(8,128)(2,1)}, u32[]{:S(2)}, u32[]{:S(2)}) %all-to-all-start.1) | async-done | bytes 14155808 | tf_op jit(solution)/shard_map/all_to_all | solution.py:20
  213.0 0.0 copy-start.1
  213.0 15.1 %fusion.14 = f32[1,1,72,128,128]{4,2,3,1,0:T(8,128)S(1)} fusion(pred[72,432]{1,0:T(8,128)(4,1)S(1)} %compare_reduce_fusion, bf16[54,8,128,128]{3,2,1,0:T(8,128)(2,1)} %bitcast.13), kind=kOutput, calls=%fused_computation.13 | convolution fusion | flops 1019215872 | bytes 18905472 | tf_op jit(solution)/shard_map/dot_general | solution.py:24
  228.2 3.0 %copy.25 = f32[1,1,72,128,128]{4,3,2,1,0:T(8,128)} copy(f32[1,1,72,128,128]{4,2,3,1,0:T(8,128)S(1)} %fusion.14) | data formatting | bytes 9437184 | tf_op jit(solution)/shard_map/dot_general | solution.py:24
  231.2 0.0 copy-done.1
  (3 shorter events, 0.0 us)
Async XLA Ops:
  0.0 22.4 %copy-start = (bf16[1,72,128,128]{3,2,1,0:T(8,128)(2,1)S(1)}, bf16[1,72,128,128]{3,2,1,0:T(8,128)(2,1)}, u32[]{:S(2)}) copy-start(bf16[1,72,128,128]{3,2,1,0:T(8,128)(2,1)} %param.6) | copy-start | bytes 7077892
  1.5 50.6 %all-to-all-start = ((s32[8,54,2]{1,2,0:T(2,128)}), s32[8,54,2]{1,2,0:T(2,128)S(1)}, u32[]{:S(2)}, u32[]{:S(2)}) async-start(s32[8,54,2]{1,2,0:T(2,128)} %copy.22), calls=%async_computation | async-start | bytes 16384 | tf_op jit(solution)/shard_map/all_to_all | solution.py:21
  52.1 6.0 %copy-start.2 = (s32[1,1,72,2]{2,3,1,0:T(2,128)S(1)}, s32[1,1,72,2]{2,3,1,0:T(2,128)}, u32[]{:S(2)}) copy-start(s32[1,1,72,2]{2,3,1,0:T(2,128)} %param.9) | copy-start | bytes 1732
  52.1 160.9 %all-to-all-start.1 = ((bf16[432,128,128]{2,1,0:T(8,128)(2,1)}), bf16[432,128,128]{2,1,0:T(8,128)(2,1)}, u32[]{:S(2)}, u32[]{:S(2)}) async-start(bf16[432,128,128]{2,1,0:T(8,128)(2,1)} %fusion.8), calls=%async_computation.1 | async-start | bytes 28311552 | tf_op jit(solution)/shard_map/all_to_all | solution.py:20
  213.0 18.2 %copy-start.1 = (bf16[1,72,128,128]{3,2,1,0:T(8,128)(2,1)S(1)}, bf16[1,72,128,128]{3,2,1,0:T(8,128)(2,1)}, u32[]{:S(2)}) copy-start(bf16[1,72,128,128]{3,2,1,0:T(8,128)(2,1)} %param.6) | copy-start | bytes 7077892
where the time goes:
time: 232 us; the launch traced here: 231 us
  waiting for transfers between devices  155 us (67%)
  local copies, waits for them, and re-layouts  32 us (14%)
  matrix products  31.6 us (14%)
  starting transfers between devices  11.9 us (5%)
    all_to_all x1, waiting for transfers between devices, device_step(): recv_vals = lax.all_to_all(part_sums, 'ksplit', 0, 0, tiled=True)  155 us
    dot_general x1, matrix products, device_step(): jnp.einsum('stab,stbc->sac', a_sel, b_sel, preferred_element_type=jnp.flo...  16.4 us
    dot_general x1, matrix products, device_step(): c_flat = jnp.dot(hit_mask, flat_vals, preferred_element_type=jnp.float32)  15.1 us
    gather x1, local copies, waits for them, and re-layouts, device_step(): a_sel = jnp.take(a_blocks, pair_tab[:, :, 0], axis=0)  14.1 us
    gather x1, local copies, waits for them, and re-layouts, device_step(): b_sel = jnp.take(b_blocks, pair_tab[:, :, 1], axis=0)  13.2 us
    all_to_all x1, starting transfers between devices, device_step(): recv_idx = lax.all_to_all(plist_loc[0, 0], 'ksplit', 0, 0, tiled=True)  6.01 us
    all_to_all x1, starting transfers between devices, device_step(): recv_vals = lax.all_to_all(part_sums, 'ksplit', 0, 0, tiled=True)  5.86 us
  transfers between devices with their start and end apart: 2, of which 1 were waited for; matrix products, arithmetic and copies ran while one was open for 19% of the time, Pallas kernels for 0%

commit v1 on v0

v1 whole, which is shorter than its diff:
```python
import functools

import jax
import jax.numpy as jnp
from jax import lax
from jax.experimental import pallas as pl
from jax.experimental.pallas import tpu as pltpu
from jax.sharding import PartitionSpec as P

MESH = pl.DeviceIdType.MESH
RING = 4
HALF_CHUNKS = (4, 5, 5)


def plan(nb):
    half = sum(HALF_CHUNKS)
    quad = (nb - 4 * half) // RING
    assert 4 * half + RING * quad == nb and quad % 2 == 0
    return half, quad


def kernel(na, nb, nc, a_hbm, b_hbm, pairs_hbm, plist_hbm, cidx_hbm, out_hbm, *scratch):
    bm, bs, am, sa = scratch[0:4], scratch[4:8], scratch[8:12], scratch[12:16]
    (meta_pairs, meta_plist, cidx, tab_v, tab_s, cacc,
     loc_sem, send_sem, recv_sem, dsend, drecv, msend, mrecv, out_sem) = scratch[16:]
    half, quad = plan(nb)
    ks = lax.axis_index("ksplit")
    y = lax.axis_index("rows")
    core = ks % 2
    x = ks // 2

    def col(dx):
        return ((x + dx) % RING) * 2 + core

    sib = {"ksplit": x * 2 + (1 - core)}
    xp, xm = {"ksplit": col(1)}, {"ksplit": col(3)}
    yp, ym = {"rows": (y + 1) % RING}, {"rows": (y + 3) % RING}

    loads = [
        pltpu.make_async_copy(pairs_hbm, meta_pairs.at[0], loc_sem.at[0]),
        pltpu.make_async_copy(plist_hbm, meta_plist.at[0], loc_sem.at[1]),
        pltpu.make_async_copy(b_hbm, bm[0], loc_sem.at[2]),
        pltpu.make_async_copy(a_hbm, am[0].at[pl.ds(0, na)], loc_sem.at[3]),
        pltpu.make_async_copy(cidx_hbm, cidx, loc_sem.at[4]),
    ]
    for load in loads:
        load.start()

    barrier = pltpu.get_barrier_semaphore()
    peers = []
    for dx in range(RING):
        for flip in range(2):
            if dx or flip:
                other = core if not flip else 1 - core
                peers.append((dx, flip, {"ksplit": ((x + dx) % RING) * 2 + other}))
    for _, _, dev in peers:
        pl.semaphore_signal(barrier, inc=1, device_id=dev, device_id_type=MESH)
    for dev in (yp, ym):
        pl.semaphore_signal(barrier, inc=1, device_id=dev, device_id_type=MESH)
    zero = jnp.zeros(am[0].shape[1:], am[0].dtype)
    for ref in (*am, *sa):
        ref[na] = zero
    pl.semaphore_wait(barrier, len(peers) + 2)

    loads[0].wait()
    loads[1].wait()
    meta = []
    for dx, flip, dev in peers:
        slot = ((RING - dx) % RING) * 2 + flip
        for n, buf in enumerate((meta_pairs, meta_plist)):
            copy = pltpu.make_async_remote_copy(
                src_ref=buf.at[0], dst_ref=buf.at[slot],
                send_sem=msend.at[2 * slot + n], recv_sem=mrecv.at[2 * slot + n],
                device_id=dev, device_id_type=MESH)
            copy.start()
            meta.append(copy)

    sems = {}
    sent = []

    def remote(key, src, dst, start, size, dev):
        if key not in sems:
            sems[key] = len(sems)
        n = sems[key]
        return pltpu.make_async_remote_copy(
            src_ref=src.at[pl.ds(start, size)], dst_ref=dst.at[pl.ds(start, size)],
            send_sem=send_sem.at[n], recv_sem=recv_sem.at[n],
            device_id=dev, device_id_type=MESH)

    def send(key, src, dst, start, size, dev):
        copy = remote(key, src, dst, start, size, dev)
        copy.start()
        sent.append(copy)

    def arrive(key, dst, start, size):
        remote(key, dst, dst, start, size, sib).wait_recv()

    def share_b(d, start, size):
        pltpu.make_async_remote_copy(
            src_ref=bm[d].at[pl.ds(start, size)], dst_ref=bs[d].at[pl.ds(start, size)],
            send_sem=dsend.at[d], recv_sem=drecv.at[d], device_id=sib, device_id_type=MESH).start()

    def share_a(d, start, size):
        pltpu.make_async_remote_copy(
            src_ref=am[d].at[pl.ds(start, size)], dst_ref=sa[d].at[pl.ds(start, size)],
            send_sem=dsend.at[4 + d], recv_sem=drecv.at[4 + d], device_id=sib, device_id_type=MESH).start()

    offs, spot = [], 0
    for size in HALF_CHUNKS:
        offs.append((spot, size))
        spot += size
    mine = (y % 2) * (2 * half)
    theirs = (1 - y % 2) * (2 * half)

    def quad_at(dy):
        return 4 * half + ((y + dy) % RING) * quad

    qh = quad // 2
    nk = len(offs)
    ah = na // 2

    loads[2].wait()
    for k, (off, size) in enumerate(offs):
        u, v = mine + off, mine + half + off
        send(("x+", "u", k), bm[0], bm[3], u, size, xp)
        send(("x-", "v", k), bm[0], bm[1], v, size, xm)
        send(("x+", "v", k), bm[0], bm[3], v, size, xp)
        send(("x-", "u", k), bm[0], bm[1], u, size, xm)
    send(("x+", "w"), bm[0], bm[3], quad_at(0), quad, xp)
    send(("x-", "w"), bm[0], bm[1], quad_at(0), quad, xm)
    share_b(0, 0, nb)
    loads[3].wait()
    share_a(0, 0, na)

    loads[4].wait()
    for copy in meta:
        copy.wait_recv()
    npart = meta_plist.shape[2]
    ckey = cidx[0:1, :] * 4096 + cidx[1:2, :]
    eye = lax.broadcasted_iota(jnp.int32, (nc, nc), 0) == lax.broadcasted_iota(jnp.int32, (nc, nc), 1)
    ccol = jnp.sum(jnp.where(eye, jnp.broadcast_to(ckey, (nc, nc)), 0), axis=1, keepdims=True)
    lane = lax.broadcasted_iota(jnp.int32, (nc, 128), 1)
    table = jnp.zeros((nc, 128), jnp.int32)
    for slot in range(2 * RING):
        pkey = meta_plist[slot, 0:1, :] * 4096 + meta_plist[slot, 1:2, :]
        pval = meta_pairs[slot, 0:1, :] * 4096 + meta_pairs[slot, 1:2, :] - na * 4096
        hit = jnp.broadcast_to(ccol, (nc, npart)) == jnp.broadcast_to(pkey, (nc, npart))
        found = jnp.sum(jnp.where(hit, jnp.broadcast_to(pval, (nc, npart)), 0), axis=1, keepdims=True) + na * 4096
        table = jnp.where(lane == 2 * slot, jnp.clip(found // 4096, 0, na), table)
        table = jnp.where(lane == 2 * slot + 1, jnp.clip(found % 4096, 0, nb - 1), table)
    tab_v[...] = table
    tab_copy = pltpu.make_async_copy(tab_v, tab_s, loc_sem.at[5])
    tab_copy.start()

    def y_send(tag, d, start, size, plus=True, minus=True):
        if plus:
            send(("y+", d) + tag, bm[d], bm[d], start, size, yp)
        if minus:
            send(("y-", d) + tag, bm[d], bm[d], start, size, ym)

    def y_arrivals(d, k):
        off, size = offs[k]
        arrive(("y+", d, "u", k), bm[d], theirs + off, size)
        share_b(d, theirs + off, size)
        arrive(("y-", d, "v", k), bm[d], theirs + half + off, size)
        share_b(d, theirs + half + off, size)

    for k, (off, size) in enumerate(offs):
        u, v = mine + off, mine + half + off
        arrive(("x+", "u", k), bm[3], u, size)
        y_send(("u", k), 3, u, size, minus=False)
        send(("f+", "u", k), bm[3], bm[2], u, size, xp)
        share_b(3, u, size)
        arrive(("x-", "v", k), bm[1], v, size)
        y_send(("v", k), 1, v, size, plus=False)
        send(("f-", "v", k), bm[1], bm[2], v, size, xm)
        share_b(1, v, size)
        arrive(("x+", "v", k), bm[3], v, size)
        y_send(("v", k), 3, v, size, plus=False)
        share_b(3, v, size)
        arrive(("x-", "u", k), bm[1], u, size)
        y_send(("u", k), 1, u, size, minus=False)
        share_b(1, u, size)
        if k:
            y_arrivals(3, k - 1)
            y_arrivals(1, k - 1)
    q0 = quad_at(0)
    arrive(("x+", "w"), bm[3], q0, quad)
    y_send(("w",), 3, q0, quad)
    send(("f+", "w"), bm[3], bm[2], q0, qh, xp)
    arrive(("x-", "w"), bm[1], q0, quad)
    y_send(("w",), 1, q0, quad)
    send(("f-", "w"), bm[1], bm[2], q0 + qh, qh, xm)
    for part in range(2):
        send(("x+", "a", part), am[0], am[3], part * ah, ah, xp)
        send(("x-", "a", 1 - part), am[0], am[1], (1 - part) * ah, ah, xm)
    share_b(3, q0, quad)
    share_b(1, q0, quad)
    y_arrivals(3, nk - 1)
    y_arrivals(1, nk - 1)

    for k, (off, size) in enumerate(offs):
        u, v = mine + off, mine + half + off
        arrive(("f+", "u", k), bm[2], u, size)
        y_send(("u", k), 2, u, size, minus=False)
        share_b(2, u, size)
        arrive(("f-", "v", k), bm[2], v, size)
        y_send(("v", k), 2, v, size, plus=False)
        share_b(2, v, size)
        if k == 0:
            for d in (3, 1):
                qm, qp = quad_at(3), quad_at(1)
                arrive(("y+", d, "w"), bm[d], qm, quad)
                send(("g+", d), bm[d], bm[d], qm, qh, yp)
                share_b(d, qm, quad)
                arrive(("y-", d, "w"), bm[d], qp, quad)
                send(("g-", d), bm[d], bm[d], qp + qh, qh, ym)
                share_b(d, qp, quad)
        else:
            y_arrivals(2, k - 1)
    arrive(("f+", "w"), bm[2], q0, qh)
    y_send(("w", 0), 2, q0, qh)
    arrive(("f-", "w"), bm[2], q0 + qh, qh)
    y_send(("w", 1), 2, q0 + qh, qh)
    share_b(2, q0, quad)

    def wait_b(d):
        pltpu.make_async_copy(bs[d], bs[d], drecv.at[d]).wait()

    def wait_a(d):
        view = sa[d].at[pl.ds(0, na)]
        pltpu.make_async_copy(view, view, drecv.at[4 + d]).wait()

    size = cacc.shape[1]

    def stage(d, first=False, last=False):
        blank = jnp.zeros((size, size), bm[0].dtype)
        group = 4

        def body(step, carry):
            for sub in range(group):
                c = step * group + sub
                lhs = jnp.concatenate([am[d][tab_s[c, 4 * d]], sa[d][tab_s[c, 4 * d + 2]]], axis=1)
                rhs = jnp.concatenate([
                    jnp.concatenate([bm[d][tab_s[c, 4 * d + 1]], blank], axis=1),
                    jnp.concatenate([blank, bs[d][tab_s[c, 4 * d + 3]]], axis=1)], axis=0)
                prod = jnp.dot(lhs, rhs, preferred_element_type=jnp.float32)
                prod = prod.astype(jnp.bfloat16).astype(jnp.float32)
                total = prod[:, :size] + prod[:, size:]
                cacc[c] = total if first else cacc[c] + total
            return carry

        if not last:
            lax.fori_loop(0, nc // group, body, 0)
            return []
        outs = []
        per = nc // 6
        for n in range(6):
            lax.fori_loop(n * per // group, (n + 1) * per // group, body, 0)
            view = pl.ds(n * per, per)
            copy = pltpu.make_async_copy(cacc.at[view], out_hbm.at[view], out_sem.at[n])
            copy.start()
            outs.append(copy)
        return outs

    tab_copy.wait()
    wait_b(0)
    wait_a(0)
    stage(0, first=True)

    for d in (3, 1):
        far = quad_at(2)
        arrive(("g+", d), bm[d], far, qh)
        arrive(("g-", d), bm[d], far + qh, qh)
        share_b(d, far, quad)
    arrive(("x+", "a", 0), am[3], 0, ah)
    send(("f+", "a"), am[3], am[2], 0, ah, xp)
    share_a(3, 0, ah)
    arrive(("x-", "a", 1), am[1], ah, ah)
    send(("f-", "a"), am[1], am[2], ah, ah, xm)
    share_a(1, ah, ah)
    y_arrivals(2, nk - 1)
    arrive(("x+", "a", 1), am[3], ah, ah)
    share_a(3, ah, ah)
    arrive(("x-", "a", 0), am[1], 0, ah)
    share_a(1, 0, ah)

    qm, qp, far = quad_at(3), quad_at(1), quad_at(2)
    arrive(("y+", 2, "w", 0), bm[2], qm, qh)
    send(("g+", 2), bm[2], bm[2], qm, qh, yp)
    arrive(("y-", 2, "w", 1), bm[2], qp + qh, qh)
    send(("g-", 2), bm[2], bm[2], qp + qh, qh, ym)
    arrive(("y+", 2, "w", 1), bm[2], qm + qh, qh)
    share_b(2, qm, quad)
    arrive(("y-", 2, "w", 0), bm[2], qp, qh)
    share_b(2, qp, quad)

    for d in (3, 1):
        wait_b(d)
        wait_a(d)
        stage(d)

    arrive(("g+", 2), bm[2], far, qh)
    arrive(("g-", 2), bm[2], far + qh, qh)
    share_b(2, far, quad)
    arrive(("f+", "a"), am[2], 0, ah)
    share_a(2, 0, ah)
    arrive(("f-", "a"), am[2], ah, ah)
    share_a(2, ah, ah)
    wait_b(2)
    wait_a(2)
    outs = stage(2, last=True)

    for copy in sent:
        copy.wait_send()
    for copy in meta:
        copy.wait_send()
    for d in range(RING):
        pltpu.make_async_copy(bm[d], bm[d], dsend.at[d]).wait()
        view = am[d].at[pl.ds(0, na)]
        pltpu.make_async_copy(view, view, dsend.at[4 + d]).wait()
    for copy in outs:
        copy.wait()


def solution(mesh):
    row_spec = P(('batch', 'rows'), 'ksplit')
    col_spec = P(('batch', 'ksplit'))
    assert mesh.shape['rows'] == RING and mesh.shape['ksplit'] == 2 * RING

    def device_step(a_loc, b_loc, pair_loc, plist_loc, cidx_loc):
        a, b = a_loc[0, 0], b_loc[0]
        pairs = pair_loc[0, 0, :, 0, :].T
        plist = plist_loc[0, 0].T
        cidx = cidx_loc[0, 0].T
        na, nb, nc, size = a.shape[0], b.shape[0], cidx.shape[1], a.shape[-1]
        npart = plist.shape[1]
        nsem = 80
        block = (size, size)
        any_spec = pl.BlockSpec(memory_space=pl.ANY)
        out = pl.pallas_call(
            functools.partial(kernel, na, nb, nc),
            out_shape=jax.ShapeDtypeStruct((nc, *block), jnp.float32),
            in_specs=[pl.BlockSpec(memory_space=pltpu.HBM)] * 5,
            out_specs=any_spec,
            scratch_shapes=[
                *[pltpu.VMEM((nb, *block), b.dtype) for _ in range(2 * RING)],
                *[pltpu.VMEM((na + 1, *block), a.dtype) for _ in range(2 * RING)],
                pltpu.VMEM((2 * RING, 2, npart), jnp.int32),
                pltpu.VMEM((2 * RING, 2, npart), jnp.int32),
                pltpu.VMEM((2, nc), jnp.int32),
                pltpu.VMEM((nc, 128), jnp.int32),
                pltpu.SMEM((nc, 128), jnp.int32),
                pltpu.VMEM((nc, *block), jnp.float32),
                pltpu.SemaphoreType.DMA((6,)),
                pltpu.SemaphoreType.DMA((nsem,)),
                pltpu.SemaphoreType.DMA((nsem,)),
                pltpu.SemaphoreType.DMA((2 * RING,)),
                pltpu.SemaphoreType.DMA((2 * RING,)),
                pltpu.SemaphoreType.DMA((4 * RING,)),
                pltpu.SemaphoreType.DMA((4 * RING,)),
                pltpu.SemaphoreType.DMA((6,)),
            ],
            compiler_params=pltpu.CompilerParams(
                collective_id=0, has_side_effects=True, vmem_limit_bytes=40 * 2**20),
        )(a, b, pairs, plist, cidx)
        return out[None, None]

    return jax.shard_map(device_step, mesh=mesh, in_specs=(row_spec, col_spec, row_spec, row_spec, row_spec), out_specs=row_spec, check_vma=False)
```

time: 232 us -> 81.6 us (0.35)
  waiting for transfers between devices: 155 us -> 0 us
  Pallas kernels: 0 us -> 74.5 us
  matrix products: 31.6 us -> 0 us
  local copies, waits for them, and re-layouts: 32 us -> 6.9 us
  starting transfers between devices: 11.9 us -> 0 us
    all_to_all x2 -> x0, waiting for transfers between devices: 155 us -> none  [the longest x1 155 us: device_step(): recv_vals = lax.all_to_all(part_sums, 'ksplit', 0, 0, tiled=True)]
    pallas_call x0 -> x1, Pallas kernels: none -> 74.5 us  [device_step(): pl.pallas_call(functools.partial(kernel, na, nb, nc), out_shape=jax.Shape...]
    dot_general x2 -> x0, matrix products: 31.6 us -> none  [the longest x1 16.4 us: device_step(): jnp.einsum('stab,stbc->sac', a_sel, b_sel, preferred_element_type=jnp.flo...]
    gather x2 -> x0, local copies, waits for them, and re-layouts: 27.3 us -> none  [the longest x1 14.1 us: device_step(): a_sel = jnp.take(a_blocks, pair_tab[:, :, 0], axis=0)]
    all_to_all x2 -> x0, starting transfers between devices: 11.9 us -> none  [the longest x1 6.01 us: device_step(): recv_idx = lax.all_to_all(plist_loc[0, 0], 'ksplit', 0, 0, tiled=True)]
    unnamed x6 -> x11, local copies, waits for them, and re-layouts: 0.01 us -> 6.9 us
    dot_general x1 -> x0, local copies, waits for them, and re-layouts: 3.04 us -> none  [device_step(): c_flat = jnp.dot(hit_mask, flat_vals, preferred_element_type=jnp.float32)]
  transfers between devices with their start and end apart: 2 -> 0, of which waited for: 1 -> 0; matrix products, arithmetic and copies ran while one was open for 19% -> 0% of each run, Pallas kernels for 0% -> 0%
where the time goes in v1:
time: 81.6 us; the launch traced here: 81.4 us
  Pallas kernels  74.5 us (91%)
  local copies, waits for them, and re-layouts  6.9 us (8%)
    pallas_call x1, Pallas kernels, device_step(): pl.pallas_call(functools.partial(kernel, na, nb, nc), out_shape=jax.Shape...  74.5 us
    unnamed x11, local copies, waits for them, and re-layouts  6.9 us

profile of v1, /device:TPU:97, one launch (start us, length us, event | category | flops | bytes accessed | tf_op | source)
XLA Modules:
  0.0 81.4 jit_solution(13115700579309243730)
XLA Ops:
  0.0 0.0 copy-start
  0.0 1.7 %copy-done = bf16[1,72,128,128]{3,2,1,0:T(8,128)(2,1)S(1)} copy-done((bf16[1,72,128,128]{3,2,1,0:T(8,128)(2,1)S(1)}, bf16[1,72,128,128]{3,2,1,0:T(8,128)(2,1)}, u32[]{:S(2)}) %copy-start) | copy-done | bytes 2359320
  1.7 0.0 copy-start.1
  1.7 1.0 %copy-done.1 = bf16[1,1,12,128,128]{4,3,2,1,0:T(8,128)(2,1)S(1)} copy-done((bf16[1,1,12,128,128]{4,3,2,1,0:T(8,128)(2,1)S(1)}, bf16[1,1,12,128,128]{4,3,2,1,0:T(8,128)(2,1)}, u32[]{:S(2)}) %copy-start.1) | copy-done | bytes 393240
  2.7 0.0 copy-start.2
  2.7 0.7 copy-done.2
  3.4 0.0 copy-start.3
  3.4 0.7 copy-done.3
  4.0 0.0 copy-start.4
  4.0 0.7 copy-done.4
  4.7 74.5 %shard_map.55 = f32[72,128,128]{2,1,0:T(8,128)S(1)} custom-call(bf16[12,128,128]{2,1,0:T(8,128)(2,1)S(1)} %bitcast.14, bf16[72,128,128]{2,1,0:T(8,128)(2,1)S(1)} %bitcast.13, s32[2,432]{1,0:T(2,128)S(1)} %bitcast.15, s32[2,432]{1,0:T(2,128)S(1)} %bitcast.16, s32[2,72]{1,0:T(2,128)S(1)} %bitcast.17), custom_call_target="tpu_custom_call" | custom-call | tf_op jit(solution)/shard_map/pallas_call | solution.py:341
  79.2 2.2 %copy.7 = f32[1,1,72,128,128]{4,3,2,1,0:T(8,128)} copy(f32[1,1,72,128,128]{4,3,2,1,0:T(8,128)S(1)} %bitcast.12) | data formatting | bytes 9437184
Async XLA Ops:
  0.0 1.7 %copy-start = (bf16[1,72,128,128]{3,2,1,0:T(8,128)(2,1)S(1)}, bf16[1,72,128,128]{3,2,1,0:T(8,128)(2,1)}, u32[]{:S(2)}) copy-start(bf16[1,72,128,128]{3,2,1,0:T(8,128)(2,1)} %param.6) | copy-start | bytes 7077892
  1.7 1.0 %copy-start.1 = (bf16[1,1,12,128,128]{4,3,2,1,0:T(8,128)(2,1)S(1)}, bf16[1,1,12,128,128]{4,3,2,1,0:T(8,128)(2,1)}, u32[]{:S(2)}) copy-start(bf16[1,1,12,128,128]{4,3,2,1,0:T(8,128)(2,1)} %param.5) | copy-start | bytes 1179652
  2.7 0.7 copy-start.2
  3.4 0.7 copy-start.3
  4.0 0.7 copy-start.4

commit v2 on v1

--- a/solution.py
+++ b/solution.py
@@ -10,6 +10,7 @@
 MESH = pl.DeviceIdType.MESH
 RING = 4
 HALF_CHUNKS = (4, 5, 5)
+GROUP = 12
 
 
 def plan(nb):
@@ -146,8 +147,8 @@
         pval = meta_pairs[slot, 0:1, :] * 4096 + meta_pairs[slot, 1:2, :] - na * 4096
         hit = jnp.broadcast_to(ccol, (nc, npart)) == jnp.broadcast_to(pkey, (nc, npart))
         found = jnp.sum(jnp.where(hit, jnp.broadcast_to(pval, (nc, npart)), 0), axis=1, keepdims=True) + na * 4096
-        table = jnp.where(lane == 2 * slot, jnp.clip(found // 4096, 0, na), table)
-        table = jnp.where(lane == 2 * slot + 1, jnp.clip(found % 4096, 0, nb - 1), table)
+        table = jnp.where(lane == 2 * slot, jnp.clip(lax.shift_right_arithmetic(found, 12), 0, na), table)
+        table = jnp.where(lane == 2 * slot + 1, jnp.clip(found & 4095, 0, nb - 1), table)
     tab_v[...] = table
     tab_copy = pltpu.make_async_copy(tab_v, tab_s, loc_sem.at[5])
     tab_copy.start()
@@ -235,7 +236,7 @@
 
     def stage(d, first=False, last=False):
         blank = jnp.zeros((size, size), bm[0].dtype)
-        group = 4
+        group = GROUP
 
         def body(step, carry):
             for sub in range(group):
@@ -362,7 +363,7 @@
                 pltpu.SemaphoreType.DMA((6,)),
             ],
             compiler_params=pltpu.CompilerParams(
-                collective_id=0, has_side_effects=True, vmem_limit_bytes=40 * 2**20),
+                collective_id=0, has_side_effects=True, vmem_limit_bytes=67043328),
         )(a, b, pairs, plist, cidx)
         return out[None, None]
 

time: 81.6 us -> 73.5 us (0.901)
  Pallas kernels: 74.5 us -> 68.2 us
  local copies, waits for them, and re-layouts: 6.9 us -> 5.09 us
    pallas_call x1, Pallas kernels: 74.5 us -> 68.2 us  [device_step(): pl.pallas_call(functools.partial(kernel, na, nb, nc), out_shape=jax.Shape...]
    unnamed x11 -> x1, local copies, waits for them, and re-layouts: 6.9 us -> 5.09 us
where the time goes in v2:
time: 73.5 us; the launch traced here: 73.3 us
  Pallas kernels  68.2 us (93%)
  local copies, waits for them, and re-layouts  5.09 us (7%)
    pallas_call x1, Pallas kernels, device_step(): pl.pallas_call(functools.partial(kernel, na, nb, nc), out_shape=jax.Shape...  68.2 us
    unnamed x1, local copies, waits for them, and re-layouts  5.09 us

profile of v2, /device:TPU:97, one launch (start us, length us, event | category | flops | bytes accessed | tf_op | source)
XLA Modules:
  0.0 73.3 jit_solution(4630872605865903829)
XLA Ops:
  0.0 68.2 %shard_map.55 = f32[72,128,128]{2,1,0:T(8,128)} custom-call(bf16[12,128,128]{2,1,0:T(8,128)(2,1)} %bitcast.14, bf16[72,128,128]{2,1,0:T(8,128)(2,1)} %bitcast.13, s32[2,432]{1,0:T(2,128)} %bitcast.15, s32[2,432]{1,0:T(2,128)} %bitcast.16, s32[2,72]{1,0:T(2,128)} %bitcast.17), custom_call_target="tpu_custom_call" | custom-call | tf_op jit(solution)/shard_map/pallas_call | solution.py:342
  68.3 5.1 %copy.7 = f32[1,1,72,128,128]{4,3,2,1,0:T(8,128)} copy(f32[1,1,72,128,128]{4,3,2,1,0:T(8,128)} %bitcast.12) | data formatting | bytes 9437184
